TPU v7x, 32 devices: a whole 2x2x4 slice. The times are simulated.
32 devices in a mesh: seq: 8 (over z, x), tp: 4 (over y, core).
Axes of the slice: x: 2, y: 2, z: 4, core: 2. Of those that a mesh axis runs over, the one named last changes fastest.
Arguments:
- queries: bfloat16 [1536, 4096], P('seq', 'tp'), may hold values from -80 to 80
- keys: bfloat16 [1536, 512], P('seq', 'tp'), may hold values from -4 to 4
- values: bfloat16 [1536, 512], P('seq', 'tp'), may hold values from -6 to 6
- segment_ids: int32 [1536], P('seq'), may hold values from 0 to 15, never falling along the last dimension, each value on 1 to 1152 neighbouring positions
- out_weight: bfloat16 [4096, 8192], P('tp', 'seq'), may hold values from -0.09375 to 0.09375
Outputs:
- projected: bfloat16 [1536, 8192], P('seq', 'tp')
Inputs may be any that keep to these rules, and one draw needn't show every extreme that they name: `segment_ids`: segment numbers never fall along the sequence and every number from 0 to 15 occurs; no document has more than 1152 tokens and one has exactly that many.
All inputs are finite; a program needn't handle non-finite values.
Results may differ from a plain program's by a relative error of at most 0.012.
Values may be sent and summed in bfloat16 or wider, within the bound.
No kernel may reach another device: no remote copies, remote signals or barrier semaphores. Data moves between devices by JAX's collectives and lax.ppermute only.
A program may use at most 128 MiB of HBM per device.

v0:
```python
import math

import jax
import jax.numpy as jnp
from jax import lax
from jax.sharding import PartitionSpec as P

HEADS = 32
KV_HEADS = 4
HEAD_DIM = 128
SEGMENTS = 16


rope_base = 500000.0
masked_score = -1e30


def rotate_heads(inputs, positions, head_dim):
    row_count = inputs.shape[0]
    head_count = inputs.shape[1] // head_dim
    half_dim = head_dim // 2
    widened = inputs.astype(jnp.float32).reshape(row_count, head_count, head_dim)
    exponent = jnp.arange(half_dim, dtype=jnp.float32) * (2.0 / head_dim)
    inverse = jnp.power(jnp.float32(rope_base), -exponent)
    angles = positions.astype(jnp.float32)[:, None] * inverse[None, :]
    cosine_table = jnp.cos(angles)[:, None, :]
    sine_table = jnp.sin(angles)[:, None, :]
    first_half = widened[:, :, :half_dim]
    second_half = widened[:, :, half_dim:]
    turned = jnp.concatenate(
        [
            first_half * cosine_table - second_half * sine_table,
            second_half * cosine_table + first_half * sine_table,
        ],
        axis=2,
    )
    return turned.reshape(row_count, head_count * head_dim).astype(jnp.bfloat16)


def doc_counts_of(segment_ids, segments):
    labels = jnp.arange(segments, dtype=jnp.int32)
    return jnp.sum((segment_ids[None, :] == labels[:, None]).astype(jnp.int32), axis=1)


def first_rows(segment, starts):
    labels = jnp.arange(starts.shape[0], dtype=jnp.int32)
    return jnp.sum(jnp.where(segment[:, None] == labels[None, :], starts[None, :], 0), axis=1)


def segment_of(global_rows, doc_ends):
    return jnp.sum((doc_ends[None, :] <= global_rows[:, None]).astype(jnp.int32), axis=1)


def block_length(piece_rows):
    for candidate in (256, 128):
        return candidate
    candidate = min(piece_rows, 256)
    while piece_rows % candidate != 0:
        candidate = candidate - 1
    return candidate


def local(queries, keys, values, segment_ids, out_weight):
    row_count = queries.shape[0]
    half_rows = row_count // 2
    my_index = lax.axis_index("seq")
    counts = doc_counts_of(segment_ids, SEGMENTS)
    totals = lax.psum(counts, "seq")
    doc_ends = jnp.cumsum(totals)
    starts = doc_ends - totals
    own_rows = my_index * row_count + jnp.arange(row_count, dtype=jnp.int32)
    positions = own_rows - first_rows(segment_ids, starts)
    query_rot = rotate_heads(queries, positions, HEAD_DIM)
    key_rot = rotate_heads(keys, positions, HEAD_DIM)
    query_segs = segment_of(own_rows, doc_ends)
    kv_local = keys.shape[1] // HEAD_DIM
    group_size = HEADS // KV_HEADS
    score_scale = 1.0 / math.sqrt(HEAD_DIM)
    query_halves = []
    for which_half in range(2):
        lower = which_half * half_rows
        query_halves.append(
            (
                query_rot[lower : lower + half_rows].reshape(
                    half_rows, kv_local, group_size, HEAD_DIM
                ),
                own_rows[lower : lower + half_rows],
                query_segs[lower : lower + half_rows],
            )
        )

    def empty_state():
        return (
            jnp.full((kv_local, group_size, half_rows), masked_score, jnp.float32),
            jnp.zeros((kv_local, group_size, half_rows), jnp.float32),
            jnp.zeros((kv_local, group_size, half_rows, HEAD_DIM), jnp.float32),
        )

    def attend_tile(carried, key_tile, value_tile, key_rows):
        key_segs = segment_of(key_rows, doc_ends)
        key_heads = key_tile.reshape(-1, kv_local, HEAD_DIM)
        value_heads = value_tile.reshape(-1, kv_local, HEAD_DIM)
        results = []
        for which_half in range(2):
            query_tile, rows_here, segs_here = query_halves[which_half]
            visible = (key_rows[None, :] <= rows_here[:, None]) & (
                key_segs[None, :] == segs_here[:, None]
            )

            def compute(running, query_tile=query_tile, visible=visible):
                row_max, normalizer, numerator = running
                scores = (
                    jnp.einsum(
                        "tkgd,skd->kgts", query_tile, key_heads, preferred_element_type=jnp.float32
                    )
                    * score_scale
                )
                scores = jnp.where(visible[None, None], scores, masked_score)
                new_max = jnp.maximum(row_max, jnp.max(scores, axis=-1))
                rescale = jnp.exp(row_max - new_max)
                weights_full = jnp.where(
                    visible[None, None], jnp.exp(scores - new_max[..., None]), 0.0
                )
                normalizer = normalizer * rescale + jnp.sum(weights_full, axis=-1)
                weights_low = weights_full.astype(jnp.bfloat16)
                numerator = numerator * rescale[..., None] + jnp.einsum(
                    "kgts,skd->kgtd", weights_low, value_heads, preferred_element_type=jnp.float32
                )
                return (new_max, normalizer, numerator)

            def keep(running):
                return running

            results.append(lax.cond(jnp.any(visible), compute, keep, carried[which_half]))
        return tuple(results)

    initial = (empty_state(), empty_state())
    key_piece = lax.all_gather(key_rot, "seq", axis=0, tiled=True)
    value_piece = lax.all_gather(values, "seq", axis=0, tiled=True)
    piece_rows = key_piece.shape[0]
    block_rows = block_length(piece_rows)

    def step(block_number, running):
        offset = block_number * block_rows
        key_tile = lax.dynamic_slice_in_dim(key_piece, offset, block_rows, 0)
        value_tile = lax.dynamic_slice_in_dim(value_piece, offset, block_rows, 0)
        key_rows = offset + jnp.arange(block_rows, dtype=jnp.int32)
        return attend_tile(running, key_tile, value_tile, key_rows)

    final = lax.fori_loop(0, piece_rows // block_rows, step, initial)
    halves_out = []
    for which_half in range(2):
        row_max, normalizer, numerator = final[which_half]
        output = numerator / normalizer[..., None]
        halves_out.append(
            jnp.transpose(output, (2, 0, 1, 3))
            .reshape(half_rows, kv_local * group_size * HEAD_DIM)
            .astype(jnp.bfloat16)
        )
    attended = jnp.concatenate(halves_out, axis=0)
    partial_value = jnp.dot(
        attended,
        lax.all_gather(out_weight, "seq", axis=1, tiled=True),
        preferred_element_type=jnp.float32,
    ).astype(jnp.bfloat16)
    summed = (
        lax.psum_scatter(partial_value, "tp", scatter_dimension=1, tiled=True)
        .astype(jnp.float32)
        .astype(jnp.bfloat16)
    )
    return summed


def solution(mesh):
    return jax.shard_map(
        local,
        mesh=mesh,
        in_specs=(P("seq", "tp"), P("seq", "tp"), P("seq", "tp"), P("seq"), P("tp", "seq")),
        out_specs=P("seq", "tp"),
        check_vma=False,
    )
```

profile of v0, /device:TPU:27, one launch (start us, length us, event | category | flops | bytes accessed | tf_op | source)
XLA Modules:
  0.0 298.5 jit_solution(15773359155438761860)
XLA Ops:
  6.5 0.7 all-gather.3.cloned.1.call-update
  7.3 0.8 convert_reduce_fusion.2
  8.1 5.6 %psum.7 = s32[16]{0:T(128)S(1)} all-reduce(s32[16]{0:T(128)S(1)} %convert_reduce_fusion.2), channel_id=1, replica_groups=mesh['seq'=8,'tp'=4] {'seq'}, use_global_device_ids=true, to_apply=%region_1.0 | all-reduce | flops 16 | bytes 128 | tf_op jit(solution)/shard_map/psum | solution.py:68
  14.0 1.1 convert_bitcast_fusion
  15.2 0.8 select_reduce_fusion
  16.0 0.4 multiply_cosine_fusion
  16.4 0.4 add_convert_fusion
  16.9 0.2 fusion.35
  17.2 0.8 bitcast_convert_fusion
  18.0 0.5 fusion.43
  18.6 30.2 %all-gather = bf16[1536,1,128]{2,0,1:T(8,128)(2,1)S(1)} all-gather(bf16[192,1,128]{2,0,1:T(8,128)(2,1)S(1)} %pad_maximum_fusion.1), channel_id=2, replica_groups=mesh['seq'=8,'tp'=4] {'seq'}, dimensions={0}, use_global_device_ids=true | all-gather | bytes 442368 | tf_op jit(solution)/shard_map/all_gather | solution.py:138
  48.8 28.3 %all_gather.10 = bf16[1536,128]{1,0:T(8,128)(2,1)S(1)} all-gather(bf16[192,128]{1,0:T(8,128)(2,1)} %param.13), channel_id=1, replica_groups=mesh['seq'=8,'tp'=4] {'seq'}, dimensions={0}, use_global_device_ids=true | all-gather | bytes 442368 | tf_op jit(solution)/shard_map/all_gather | solution.py:139
  77.3 16.5 %while.23 = (s32[]{:T(128)}, f32[1,8,96]{2,1,0:T(8,128)S(1)}, f32[1,8,96]{2,1,0:T(8,128)S(1)}, f32[1,8,96,128]{3,2,1,0:T(8,128)S(1)}, f32[1,8,96]{2,1,0:T(8,128)...) while((s32[]{:T(128)}, f32[1,8,96]{2,1,0:T(8,128)S(1)}, ...), condition=%wide.region_17.18_spmd, body=%wide.region_5.17_spmd.sunk | while | flops 205472256 | bytes 7511063 | solution.py:150
  77.4 0.8 fusion.55
  79.8 0.8 fusion.55
  82.1 0.8 fusion.55
  84.4 0.8 fusion.55
  86.8 0.8 fusion.55
  89.1 0.8 fusion.55
  91.3 1.2 conditional.4
  91.3 0.4 fusion.49
  91.7 0.4 fusion.4
  92.1 0.4 fusion.2
  92.5 1.2 conditional.5
  92.5 0.4 fusion.50
  93.0 0.4 fusion.19
  93.3 0.4 fusion.17
  93.8 0.2 fusion.37
  94.1 0.2 fusion.36
  94.4 147.8 %all-gather.3.cloned.1.call-done = bf16[1024,8192]{1,0:T(8,128)(2,1)} async-done(((bf16[1024,1024]{1,0:T(8,128)(2,1)}), bf16[1024,8192]{1,0:T(8,128)(2,1)}) %all-gather.3.cloned.1.call-update) | async-done | bytes 16777232 | tf_op jit(solution)/shard_map/all_gather | solution.py:163
  242.2 10.9 %convolution_convert_fusion = bf16[192,8192]{1,0:T(8,128)(2,1)} fusion(bf16[1024,8192]{1,0:T(8,128)(2,1)} %all-gather.3.cloned.1.call-done, bf16[96,1024]{1,0:T(8,128)(2,1)S(1)} %bitcast.119, bf16[96,1024]{1,0:T(8,128)(2,1)S(1)} %bitcast.120), kind=kOutput, calls=%fused_computation.46 | convolution fusion | flops 3223584768 | bytes 20316160 | tf_op jit(solution)/shard_map/dot_general | solution.py:161
  253.1 38.7 %reduce-scatter.2.cloned.1.call-done = bf16[192,2048]{1,0:T(8,128)(2,1)} async-done(((bf16[192,8192]{1,0:T(8,128)(2,1)}), bf16[192,2048]{1,0:T(8,128)(2,1)}) %reduce-scatter.2.cloned.1.call-update) | async-done | bytes 786448 | tf_op jit(solution)/shard_map/reduce_scatter | solution.py:167
  (60 shorter events, 2.0 us)
Async XLA Ops:
  6.5 235.6 %all-gather.3.cloned.1.call-start = ((), (), s32[]{:S(2)}) async-start(), calls=%async_computation.1 | async-start | bytes 18874368 | tf_op jit(solution)/shard_map/all_gather | solution.py:163
  7.3 284.5 %reduce-scatter.2.cloned.1.call-start = ((), (), s32[]{:S(2)}) async-start(), calls=%async_computation.2 | async-start | bytes 3932160 | tf_op jit(solution)/shard_map/reduce_scatter | solution.py:167
Sparse Core Ops, SparseCore 0:
  9.5 232.5 all-gather.2
  253.2 38.4 reduce-scatter.1
where the time goes:
time: 301 us; the launch traced here: 299 us
  waiting for transfers between devices  187 us (62%)
  blocking collectives  64.1 us (21%)
  between operations  13.5 us (4%)
  matrix products  12.4 us (4%)
  other arithmetic  12 us (4%)
  loops' own time  8.45 us (3%)
    all_gather x1, waiting for transfers between devices, local(): lax.all_gather(out_weight, 'seq', axis=1, tiled=True)  148 us
    reduce_scatter x1, waiting for transfers between devices, local(): lax.psum_scatter(partial_value, 'tp', scatter_dimension=1, tiled=True)  38.7 us
    all_gather x1, blocking collectives, local(): key_piece = lax.all_gather(key_rot, 'seq', axis=0, tiled=True)  30.2 us
    all_gather x1, blocking collectives, local(): value_piece = lax.all_gather(values, 'seq', axis=0, tiled=True)  28.3 us
    dot_general x1, matrix products, local(): jnp.dot(attended, lax.all_gather(out_weight, 'seq', axis=1, tiled=True),...  10.9 us
    another operation x1, loops' own time, local(): final = lax.fori_loop(0, piece_rows // block_rows, step, initial)  8.16 us
  transfers between devices with their start and end apart: 2, of which 2 were waited for; matrix products, arithmetic and copies ran while one was open for 5% of the time, Pallas kernels for 0%

commit v1 on v0

v1 whole, which is shorter than its diff:
```python
import functools
import math

import jax
import jax.numpy as jnp
from jax import lax
from jax.experimental import pallas as pl
from jax.experimental.pallas import tpu as pltpu
from jax.sharding import Mesh, PartitionSpec as P

HEADS = 32
KV_HEADS = 4
HEAD_DIM = 128
SEGMENTS = 16

rope_base = 500000.0
masked_score = -1e30
INFO_ROWS = 16
BASE = 128


def doc_counts_of(segment_ids, segments):
    labels = jnp.arange(segments, dtype=jnp.int32)
    return jnp.sum((segment_ids[None, :] == labels[:, None]).astype(jnp.int32), axis=1)


def largest_divisor(total, candidates):
    for candidate in candidates:
        if total % candidate == 0:
            return candidate
    return total


def rotary_tables(positions):
    half = HEAD_DIM // 2
    exponent = jnp.arange(half, dtype=jnp.float32) * (2.0 / HEAD_DIM)
    inverse = jnp.power(jnp.float32(rope_base), -exponent)
    angles = positions.astype(jnp.float32)[:, None] * inverse[None, :]
    cosine = jnp.cos(angles)
    sine = jnp.sin(angles)
    return (
        jnp.concatenate([cosine, cosine], axis=1),
        jnp.concatenate([-sine, sine], axis=1),
    )


def attend_kernel(
    scalars,
    queries,
    cosine,
    sine,
    keys,
    values,
    out,
    stacked,
    top,
    total,
    numerator,
    *,
    tile_q,
    tile_k,
    heads,
    segments,
):
    tile = pl.program_id(0)
    first = scalars[0] + tile * tile_q
    low = jnp.int32(0)
    for g in range(segments):
        end = scalars[1 + g]
        low = jnp.maximum(low, jnp.where(end <= first, end, 0))
    rows = first + lax.broadcasted_iota(jnp.int32, (tile_q, tile_k), 0)
    starts = jnp.zeros((tile_q, tile_k), jnp.int32)
    for g in range(segments):
        end = scalars[1 + g]
        starts = jnp.maximum(starts, jnp.where(end <= rows, end, 0))
    cos_tile = cosine[...]
    sin_tile = sine[...]
    for h in range(heads):
        x = queries[:, h * HEAD_DIM : (h + 1) * HEAD_DIM].astype(jnp.float32)
        turned = x * cos_tile + pltpu.roll(x, HEAD_DIM // 2, 1) * sin_tile
        stacked[h * tile_q : (h + 1) * tile_q, :] = turned.astype(jnp.bfloat16)
    top[...] = jnp.full(top.shape, masked_score, jnp.float32)
    total[...] = jnp.zeros(total.shape, jnp.float32)
    numerator[...] = jnp.zeros(numerator.shape, jnp.float32)
    scale = math.log2(math.e) / math.sqrt(HEAD_DIM)
    last_tile = (first + tile_q - 1) // tile_k
    first_tile = low // tile_k
    lanes = lax.broadcasted_iota(jnp.int32, (tile_q, tile_k), 1)

    def step(index, carry):
        offset = pl.multiple_of((last_tile - index) * tile_k, tile_k)
        key_tile = keys[pl.ds(offset, tile_k), :]
        value_tile = values[pl.ds(offset, tile_k), :]
        scores = lax.dot_general(
            stacked[...], key_tile, (((1,), (1,)), ((), ())), preferred_element_type=jnp.float32
        )
        columns = offset + lanes
        visible = (columns <= rows) & (columns >= starts)
        scores = jnp.where(visible[None], scores.reshape(heads, tile_q, tile_k), masked_score)
        scores = scores.reshape(heads * tile_q, tile_k)
        old = top[...]
        new = jnp.maximum(old, jnp.max(scores, axis=1, keepdims=True))
        rescale = jnp.exp2((old - new) * scale)
        weights = jnp.exp2((scores - new) * scale)
        total[...] = total[...] * rescale + jnp.sum(weights, axis=1, keepdims=True)
        numerator[...] = numerator[...] * rescale + jnp.dot(
            weights.astype(jnp.bfloat16), value_tile, preferred_element_type=jnp.float32
        )
        top[...] = new
        return carry

    lax.fori_loop(0, last_tile - first_tile + 1, step, 0)
    result = numerator[...] / total[...]
    for h in range(heads):
        out[:, h * HEAD_DIM : (h + 1) * HEAD_DIM] = result[h * tile_q : (h + 1) * tile_q, :].astype(
            jnp.bfloat16
        )


def attend(scalars, queries, cosine, sine, keys, values):
    row_count, width = queries.shape
    heads = width // HEAD_DIM
    key_count = keys.shape[0]
    tile_q = largest_divisor(row_count, (64, 32, 16))
    tile_k = largest_divisor(key_count, (256, 128))
    segments = scalars.shape[0] - 1
    kernel = functools.partial(
        attend_kernel, tile_q=tile_q, tile_k=tile_k, heads=heads, segments=segments
    )
    whole = pl.BlockSpec((key_count, HEAD_DIM), lambda i, s: (0, 0))
    pairs = row_count * key_count * heads // 3
    return pl.pallas_call(
        kernel,
        out_shape=jax.ShapeDtypeStruct((row_count, width), jnp.bfloat16),
        grid_spec=pltpu.PrefetchScalarGridSpec(
            num_scalar_prefetch=1,
            grid=(row_count // tile_q,),
            in_specs=[
                pl.BlockSpec((tile_q, width), lambda i, s: (i, 0)),
                pl.BlockSpec((tile_q, HEAD_DIM), lambda i, s: (i, 0)),
                pl.BlockSpec((tile_q, HEAD_DIM), lambda i, s: (i, 0)),
                whole,
                whole,
            ],
            out_specs=pl.BlockSpec((tile_q, width), lambda i, s: (i, 0)),
            scratch_shapes=[
                pltpu.VMEM((heads * tile_q, HEAD_DIM), jnp.bfloat16),
                pltpu.VMEM((heads * tile_q, 1), jnp.float32),
                pltpu.VMEM((heads * tile_q, 1), jnp.float32),
                pltpu.VMEM((heads * tile_q, HEAD_DIM), jnp.float32),
            ],
        ),
        cost_estimate=pl.CostEstimate(
            flops=4 * pairs * HEAD_DIM,
            bytes_accessed=4 * row_count * width + 4 * key_count * HEAD_DIM,
            transcendentals=pairs,
        ),
        name="attend",
    )(scalars, queries, cosine, sine, keys, values)


def local(queries, keys, values, segment_ids, out_weight, *, outer, inner, groups):
    row_count = queries.shape[0]
    width = queries.shape[1]
    z = lax.axis_index("outer")
    x = lax.axis_index("inner")
    k = lax.axis_index("tp")

    counts = doc_counts_of(segment_ids, SEGMENTS)
    info = jnp.concatenate([counts // BASE, counts % BASE]).astype(jnp.bfloat16)
    info = jnp.pad(info[None, :], ((0, INFO_ROWS - 1), (0, HEAD_DIM - 2 * SEGMENTS)))
    own = jnp.concatenate([keys, values, info], axis=0)
    block_rows = own.shape[0]

    def shift(array, axis, size, distance):
        pairs = [(i, (i - distance) % size) for i in range(size)]
        return lax.ppermute(array, axis, pairs)

    near = jnp.zeros((inner, block_rows, HEAD_DIM), jnp.bfloat16)
    near = lax.dynamic_update_slice(near, own[None], (x, 0, 0))
    for d in range(1, inner):
        got = shift(own, "inner", inner, d)
        near = lax.dynamic_update_slice(near, got[None], ((x + d) % inner, 0, 0))
    weights = [out_weight]
    for d in range(1, inner):
        weights.append(shift(out_weight, "inner", inner, d))

    every = jnp.zeros((outer, inner, block_rows, HEAD_DIM), jnp.bfloat16)
    every = lax.dynamic_update_slice(every, near[None], (z, 0, 0, 0))
    for d in range(1, outer):
        got = shift(near, "outer", outer, d)
        every = lax.dynamic_update_slice(every, got[None], ((z + d) % outer, 0, 0, 0))
    every = every.reshape(outer * inner, block_rows, HEAD_DIM)
    query_blocks = [queries] + [shift(queries, "outer", outer, d) for d in range(1, outer)]

    info = every[:, 2 * row_count, :].astype(jnp.float32)
    block_counts = info[:, :SEGMENTS] * BASE + info[:, SEGMENTS : 2 * SEGMENTS]
    totals = jnp.sum(block_counts, axis=0).astype(jnp.int32)
    labels = jnp.arange(SEGMENTS, dtype=jnp.int32)
    doc_ends = jnp.sum(jnp.where(labels[None, :] <= labels[:, None], totals[None, :], 0), axis=1)
    token_count = outer * inner * row_count
    tokens = jnp.arange(token_count, dtype=jnp.int32)
    doc_starts = jnp.max(
        jnp.where(doc_ends[None, :] <= tokens[:, None], doc_ends[None, :], 0), axis=1
    )
    cosine, sine = rotary_tables(tokens - doc_starts)
    raw_keys = every[:, :row_count, :].reshape(token_count, HEAD_DIM).astype(jnp.float32)
    swapped = jnp.concatenate([raw_keys[:, HEAD_DIM // 2 :], raw_keys[:, : HEAD_DIM // 2]], axis=1)
    key_rot = (raw_keys * cosine + swapped * sine).astype(jnp.bfloat16)
    value_all = every[:, row_count : 2 * row_count, :].reshape(token_count, HEAD_DIM)

    attended = []
    for d in range(outer):
        first = (((z + d) % outer) * inner + x) * row_count
        scalars = jnp.concatenate([first[None].astype(jnp.int32), doc_ends])
        cos_rows = lax.dynamic_slice_in_dim(cosine, first, row_count, 0)
        sin_rows = lax.dynamic_slice_in_dim(sine, first, row_count, 0)
        attended.append(attend(scalars, query_blocks[d], cos_rows, sin_rows, key_rot, value_all))
    attended = jnp.stack(attended)

    def project(weight):
        blocks = attended
        bit = 1
        size = groups
        partial = None
        while bit < groups:
            mine = (k // bit) % 2
            if partial is None:
                paired = blocks.reshape(size // 2, 2, row_count, width)
                give = lax.dynamic_index_in_dim(paired, 1 - mine, 1, keepdims=False)
                keep = lax.dynamic_index_in_dim(paired, mine, 1, keepdims=False)

                def times(rows):
                    flat = rows.reshape(-1, width)
                    return jnp.dot(flat, weight, preferred_element_type=jnp.float32)

                given = times(give).astype(jnp.bfloat16)
                kept = times(keep)
            else:
                paired = partial.reshape(size // 2, 2, row_count, -1)
                give = lax.dynamic_index_in_dim(paired, 1 - mine, 1, keepdims=False)
                kept = lax.dynamic_index_in_dim(paired, mine, 1, keepdims=False)
                given = give.astype(jnp.bfloat16).reshape(size // 2 * row_count, -1)
                kept = kept.reshape(size // 2 * row_count, -1)
            got = lax.ppermute(given, "tp", [(i, i ^ bit) for i in range(groups)])
            partial = kept.astype(jnp.bfloat16).astype(jnp.float32) + got.astype(jnp.float32)
            size = size // 2
            bit = bit * 2
        moves = []
        for a in range(outer):
            for b in range(groups):
                moves.append((a * groups + b, ((a + b) % outer) * groups + a))
        return lax.ppermute(partial.astype(jnp.bfloat16), ("outer", "tp"), moves)

    pieces = [project(weights[0])]
    if inner > 1:
        pieces.append(project(jnp.concatenate(weights[1:], axis=1)))
    relative = jnp.concatenate(pieces, axis=1)
    if inner == 1:
        return relative
    columns = out_weight.shape[1]
    if inner == 2:
        turned = jnp.concatenate([relative[:, columns:], relative[:, :columns]], axis=1)
        return jnp.where(x == 0, relative, turned)
    doubled = jnp.concatenate([relative, relative], axis=1)
    offset = ((inner - x) % inner) * columns
    return lax.dynamic_slice_in_dim(doubled, offset, inner * columns, 1)


def solution(mesh):
    seq, groups = mesh.shape["seq"], mesh.shape["tp"]
    outer, inner = groups, seq // groups
    split = Mesh(mesh.devices.reshape(outer, inner, groups), ("outer", "inner", "tp"))
    whole = ("outer", "inner")
    return jax.shard_map(
        functools.partial(local, outer=outer, inner=inner, groups=groups),
        mesh=split,
        in_specs=(P(whole, "tp"), P(whole, "tp"), P(whole, "tp"), P(whole), P("tp", whole)),
        out_specs=P(whole, "tp"),
        check_vma=False,
    )
```

time: 301 us -> 176 us (0.58); the launches traced: 299 us -> 179 us
  waiting for transfers between devices: 187 us -> 67.7 us
  blocking collectives: 64.1 us -> 0 us
  Pallas kernels: 0 us -> 59.2 us
  starting transfers between devices: 0.04 us -> 26.4 us
  between operations: 13.5 us -> 0.29 us
  loops' own time: 8.45 us -> 0 us
  matrix products: 12.4 us -> 7.29 us
  local copies, waits for them, and re-layouts: 0.83 us -> 5.23 us
    all_gather x1 -> x0, waiting for transfers between devices: 148 us -> none  [local(): lax.all_gather(out_weight, 'seq', axis=1, tiled=True)]
    ppermute x0 -> x14, waiting for transfers between devices: none -> 67.7 us  [the longest x8 40.5 us: shift(): return lax.ppermute(array, axis, pairs)]
    pallas_call x0 -> x4, Pallas kernels: none -> 59.2 us  [attend(): pl.pallas_call(kernel, out_shape=jax.ShapeDtypeStruct((row_count, width),...]
    all_gather x2 -> x0, blocking collectives: 58.4 us -> none  [the longest x1 30.2 us: local(): key_piece = lax.all_gather(key_rot, 'seq', axis=0, tiled=True)]
    reduce_scatter x1 -> x0, waiting for transfers between devices: 38.7 us -> none  [local(): lax.psum_scatter(partial_value, 'tp', scatter_dimension=1, tiled=True)]
    ppermute x0 -> x14, starting transfers between devices: none -> 26.4 us  [the longest x8 11.7 us: shift(): return lax.ppermute(array, axis, pairs)]
    another operation x13 -> x0, loops' own time: 8.45 us -> none  [the longest x1 8.16 us: local(): final = lax.fori_loop(0, piece_rows // block_rows, step, initial)]
    psum x1 -> x0, blocking collectives: 5.62 us -> none  [local(): totals = lax.psum(counts, 'seq')]
  transfers between devices with their start and end apart: 2 -> 14, of which waited for: 2 -> 8; matrix products, arithmetic and copies ran while one was open for 5% -> 11% of each run, Pallas kernels for 0% -> 33%
where the time goes in v1:
time: 176 us; the launch traced here: 179 us
  waiting for transfers between devices  67.7 us (38%)
  Pallas kernels  59.2 us (34%)
  starting transfers between devices  26.4 us (15%)
  other arithmetic  12.6 us (7%)
  matrix products  7.29 us (4%)
  local copies, waits for them, and re-layouts  5.23 us (3%)
    pallas_call x4, Pallas kernels, attend(): pl.pallas_call(kernel, out_shape=jax.ShapeDtypeStruct((row_count, width),...  59.2 us
    ppermute x8, waiting for transfers between devices, shift(): return lax.ppermute(array, axis, pairs)  40.5 us
    ppermute x2, waiting for transfers between devices, project(): return lax.ppermute(partial.astype(jnp.bfloat16), ('outer', 'tp'), moves)  14.6 us
    ppermute x4, waiting for transfers between devices, project(): got = lax.ppermute(given, 'tp', [(i, i ^ bit) for i in range(groups)])  12.5 us
    ppermute x8, starting transfers between devices, shift(): return lax.ppermute(array, axis, pairs)  11.7 us
    ppermute x2, starting transfers between devices, project(): return lax.ppermute(partial.astype(jnp.bfloat16), ('outer', 'tp'), moves)  10.4 us
    dot_general x4, matrix products, times(): return jnp.dot(flat, weight, preferred_element_type=jnp.float32)  7.29 us
    ppermute x4, starting transfers between devices, project(): got = lax.ppermute(given, 'tp', [(i, i ^ bit) for i in range(groups)])  4.18 us
  transfers between devices with their start and end apart: 14, of which 8 were waited for; matrix products, arithmetic and copies ran while one was open for 11% of the time, Pallas kernels for 33%

profile of v1, /device:TPU:27, one launch (start us, length us, event | category | flops | bytes accessed | tf_op | source)
XLA Modules:
  0.0 178.7 jit_solution(4111022890146933839)
XLA Ops:
  0.2 3.0 %collective-permute-start.6 = (bf16[192,1024]{1,0:T(8,128)(2,1)}, bf16[192,1024]{1,0:T(8,128)(2,1)S(1)}, u32[]{:S(2)}, u32[]{:S(2)}) collective-permute-start(bf16[192,1024]{1,0:T(8,128)(2,1)} %queries.1), channel_id=1, source_target_pairs={{0,8},{8,16},{16,24},{24,0},{1,9},{9,17},{17,25},{25,1},{2,10},{10... | collective-permute-start | bytes 1179656 | tf_op jit(solution)/shard_map/ppermute | solution.py:177
  4.2 0.8 pad_maximum_fusion.1
  5.3 1.2 collective-permute-start.10
  6.5 0.8 bitcast_dynamic-update-slice_fusion.5
  7.5 1.4 collective-permute-done
  9.4 24.1 %collective-permute-done.1 = bf16[2,400,128]{2,1,0:T(8,128)(2,1)S(1)} collective-permute-done((bf16[2,400,128]{2,1,0:T(8,128)(2,1)S(1)}, bf16[2,400,128]{2,1,0:T(8,128)(2,1)S(1)}, u32[]{:S(2)}, u32[]{:S(2)}) %collective-permute-start.1) | collective-permute-done | bytes 204832 | tf_op jit(solution)/shard_map/ppermute | solution.py:177
  33.4 6.6 %collective-permute-start.2 = (bf16[2,400,128]{2,1,0:T(8,128)(2,1)S(1)}, bf16[2,400,128]{2,1,0:T(8,128)(2,1)S(1)}, u32[]{:S(2)}, u32[]{:S(2)}) collective-permute-start(bf16[2,400,128]{2,1,0:T(8,128)(2,1)S(1)} %bitcast_dynamic-update-slice_fusion.4), channel_id=1, source_target_pairs={{0,16},{8,24},{16,0},{24,8},{1,17},{9,25},{17,1},{25,9},{2,18},{10... | collective-permute-start | bytes 614408 | tf_op jit(solution)/shard_map/ppermute | solution.py:177
  40.1 10.0 %collective-permute-done.2 = bf16[2,400,128]{2,1,0:T(8,128)(2,1)S(1)} collective-permute-done((bf16[2,400,128]{2,1,0:T(8,128)(2,1)S(1)}, bf16[2,400,128]{2,1,0:T(8,128)(2,1)S(1)}, u32[]{:S(2)}, u32[]{:S(2)}) %collective-permute-start.2) | collective-permute-done | bytes 204832 | tf_op jit(solution)/shard_map/ppermute | solution.py:177
  50.1 5.1 %collective-permute-done.3 = bf16[2,400,128]{2,1,0:T(8,128)(2,1)S(1)} collective-permute-done((bf16[2,400,128]{2,1,0:T(8,128)(2,1)S(1)}, bf16[2,400,128]{2,1,0:T(8,128)(2,1)S(1)}, u32[]{:S(2)}, u32[]{:S(2)}) %collective-permute-start.3) | collective-permute-done | bytes 204832 | tf_op jit(solution)/shard_map/ppermute | solution.py:177
  56.4 2.8 %multiply_sine_fusion = (f32[1536,64]{1,0:T(8,128)S(1)}, f32[1536,64]{1,0:T(8,128)S(1)}, f32[1536,64]{1,0:T(8,128)S(1)}) fusion(f32[64]{0:T(128)S(1)} %negate_power_fusion, f32[1536]{0:T(1024)S(1)} %subtract_convert_fusion), kind=kLoop, calls=%fused_computation.7 | loop fusion | flops 196608 | bytes 1186048 | tf_op jit(solution)/shard_map/sin | solution.py:40
  59.5 1.5 fusion.1.keys
  61.6 0.9 fusion.9
  62.6 0.9 fusion.13
  63.4 22.2 %attend.4 = bf16[192,1024]{1,0:T(8,128)(2,1)} custom-call(s32[17]{0:T(128)} %get-tuple-element.22.scalars, bf16[192,1024]{1,0:T(8,128)(2,1)} %queries.1, f32[192,128]{1,0:T(8,128)} %get-tuple-element.13.cosine, f32[192,128]{1,0:T(8,128)} %get-tuple-element.7.sine, bf16[1536,128]{1,0:T(8,128)(2,1)} %fusion.1.keys, bf16[1536,128]{1,0:T(8,128)(2,1)} %bitcast.59), custom_call_target="tpu_custom_call" | custom-call | flops 402653184 | bytes 1572864 | tf_op jit(solution)/shard_map/attend/pallas_call | solution.py:132
  86.4 8.6 %attend.5 = bf16[192,1024]{1,0:T(8,128)(2,1)} custom-call(s32[17]{0:T(128)} %get-tuple-element.23.scalars, bf16[192,1024]{1,0:T(8,128)(2,1)} %copy-done.5, f32[192,128]{1,0:T(8,128)} %get-tuple-element.16.cosine, f32[192,128]{1,0:T(8,128)} %get-tuple-element.8.sine, bf16[1536,128]{1,0:T(8,128)(2,1)} %fusion.1.keys, bf16[1536,128]{1,0:T(8,128)(2,1)} %bitcast.60), custom_call_target="tpu_custom_call" | custom-call | flops 402653184 | bytes 1572864 | tf_op jit(solution)/shard_map/attend/pallas_call | solution.py:132
  95.8 11.2 %attend.6 = bf16[192,1024]{1,0:T(8,128)(2,1)} custom-call(s32[17]{0:T(128)} %get-tuple-element.24.scalars, bf16[192,1024]{1,0:T(8,128)(2,1)} %copy-done.4, f32[192,128]{1,0:T(8,128)} %get-tuple-element.14.cosine, f32[192,128]{1,0:T(8,128)} %get-tuple-element.9.sine, bf16[1536,128]{1,0:T(8,128)(2,1)} %fusion.1.keys, bf16[1536,128]{1,0:T(8,128)(2,1)} %bitcast.61), custom_call_target="tpu_custom_call" | custom-call | flops 402653184 | bytes 1572864 | tf_op jit(solution)/shard_map/attend/pallas_call | solution.py:132
  107.8 17.2 %attend.7 = bf16[192,1024]{1,0:T(8,128)(2,1)} custom-call(s32[17]{0:T(128)} %get-tuple-element.25.scalars, bf16[192,1024]{1,0:T(8,128)(2,1)} %copy-done.3, f32[192,128]{1,0:T(8,128)} %get-tuple-element.15.cosine, f32[192,128]{1,0:T(8,128)} %get-tuple-element.10.sine, bf16[1536,128]{1,0:T(8,128)(2,1)} %fusion.1.keys, bf16[1536,128]{1,0:T(8,128)(2,1)} %bitcast.62), custom_call_target="tpu_custom_call" | custom-call | flops 402653184 | bytes 1572864 | tf_op jit(solution)/shard_map/attend/pallas_call | solution.py:132
  125.0 1.2 pad_maximum_fusion
  126.3 1.4 copy-done.6
  127.8 1.0 convolution_convert_fusion.2
  128.8 2.5 %collective-permute-start.7 = (bf16[384,1024]{1,0:T(8,128)(2,1)S(1)}, bf16[384,1024]{1,0:T(8,128)(2,1)S(1)}, u32[]{:S(2)}, u32[]{:S(2)}) collective-permute-start(bf16[384,1024]{1,0:T(8,128)(2,1)S(1)} %convolution_convert_fusion.2), channel_id=1, source_target_pairs={{0,1},{1,0},{2,3},{3,2},{4,5},{5,4},{6,7},{7,6},{8,9},{9,8},{10,11... | collective-permute-start | bytes 2359304 | tf_op jit(solution)/shard_map/ppermute | solution.py:245
  131.2 2.7 %convolution_convert_fusion = bf16[384,1024]{1,0:T(8,128)(2,1)S(1)} fusion(bf16[384,1024]{1,0:T(8,128)(2,1)S(1)} %bitcast.75, bf16[1024,1024]{1,0:T(8,128)(2,1)} %collective-permute-done.10), kind=kOutput, calls=%fused_computation.3 | convolution fusion | flops 805699584 | bytes 3670016 | tf_op jit(solution)/shard_map/dot_general | solution.py:235
  134.1 1.0 convert_add_fusion.1
  135.1 1.3 collective-permute-start.8
  136.5 2.6 %convolution_convert_fusion.1 = bf16[384,1024]{1,0:T(8,128)(2,1)S(1)} fusion(bf16[384,1024]{1,0:T(8,128)(2,1)S(1)} %bitcast.73, bf16[1024,1024]{1,0:T(8,128)(2,1)} %collective-permute-done.10), kind=kOutput, calls=%fused_computation.4 | convolution fusion | flops 805699584 | bytes 3670016 | tf_op jit(solution)/shard_map/dot_general | solution.py:235
  139.7 5.8 %collective-permute-done.8 = bf16[192,1024]{1,0:T(8,128)(2,1)S(1)} collective-permute-done((bf16[192,1024]{1,0:T(8,128)(2,1)S(1)}, bf16[192,1024]{1,0:T(8,128)(2,1)S(1)}, u32[]{:S(2)}, u32[]{:S(2)}) %collective-permute-start.8) | collective-permute-done | bytes 393248 | tf_op jit(solution)/shard_map/ppermute | solution.py:245
  145.6 4.7 %collective-permute-start.9 = (bf16[192,1024]{1,0:T(8,128)(2,1)S(1)}, bf16[192,1024]{1,0:T(8,128)(2,1)S(1)}, u32[]{:S(2)}, u32[]{:S(2)}) collective-permute-start(bf16[192,1024]{1,0:T(8,128)(2,1)S(1)} %fusion.3), channel_id=1, source_target_pairs={{0,0},{1,8},{2,16},{3,24},{8,9},{9,17},{10,25},{11,1},{16,18},{17,... | collective-permute-start | bytes 1179656 | tf_op jit(solution)/shard_map/ppermute | solution.py:253
  150.3 6.7 %collective-permute-done.12 = bf16[192,1024]{1,0:T(8,128)(2,1)S(1)} collective-permute-done((bf16[192,1024]{1,0:T(8,128)(2,1)S(1)}, bf16[192,1024]{1,0:T(8,128)(2,1)S(1)}, u32[]{:S(2)}, u32[]{:S(2)}) %collective-permute-start.12) | collective-permute-done | bytes 393248 | tf_op jit(solution)/shard_map/ppermute | solution.py:245
  157.1 5.8 %collective-permute-start.13 = (bf16[192,1024]{1,0:T(8,128)(2,1)S(1)}, bf16[192,1024]{1,0:T(8,128)(2,1)S(1)}, u32[]{:S(2)}, u32[]{:S(2)}) collective-permute-start(bf16[192,1024]{1,0:T(8,128)(2,1)S(1)} %fusion.2), channel_id=1, source_target_pairs={{0,0},{1,8},{2,16},{3,24},{8,9},{9,17},{10,25},{11,1},{16,18},{17,... | collective-permute-start | bytes 1179656 | tf_op jit(solution)/shard_map/ppermute | solution.py:253
  162.9 2.0 %collective-permute-done.9 = bf16[192,1024]{1,0:T(8,128)(2,1)S(1)} collective-permute-done((bf16[192,1024]{1,0:T(8,128)(2,1)S(1)}, bf16[192,1024]{1,0:T(8,128)(2,1)S(1)}, u32[]{:S(2)}, u32[]{:S(2)}) %collective-permute-start.9) | collective-permute-done | bytes 393248 | tf_op jit(solution)/shard_map/ppermute | solution.py:253
  164.9 12.6 %collective-permute-done.13 = bf16[192,1024]{1,0:T(8,128)(2,1)S(1)} collective-permute-done((bf16[192,1024]{1,0:T(8,128)(2,1)S(1)}, bf16[192,1024]{1,0:T(8,128)(2,1)S(1)}, u32[]{:S(2)}, u32[]{:S(2)}) %collective-permute-start.13) | collective-permute-done | bytes 393248 | tf_op jit(solution)/shard_map/ppermute | solution.py:253
  177.5 1.2 maximum_select_fusion
  (55 shorter events, 7.6 us)
Async XLA Ops:
  0.0 85.7 %collective-permute-start.4 = (bf16[192,1024]{1,0:T(8,128)(2,1)}, bf16[192,1024]{1,0:T(8,128)(2,1)S(1)}, u32[]{:S(2)}, u32[]{:S(2)}) collective-permute-start(bf16[192,1024]{1,0:T(8,128)(2,1)} %queries.1), channel_id=1, source_target_pairs={{0,24},{8,0},{16,8},{24,16},{1,25},{9,1},{17,9},{25,17},{2,26},{10... | collective-permute-start | bytes 1179656 | tf_op jit(solution)/shard_map/ppermute | solution.py:177
  0.2 94.9 %collective-permute-start.5 = (bf16[192,1024]{1,0:T(8,128)(2,1)}, bf16[192,1024]{1,0:T(8,128)(2,1)S(1)}, u32[]{:S(2)}, u32[]{:S(2)}) collective-permute-start(bf16[192,1024]{1,0:T(8,128)(2,1)} %queries.1), channel_id=1, source_target_pairs={{0,16},{8,24},{16,0},{24,8},{1,17},{9,25},{17,1},{25,9},{2,18},{10... | collective-permute-start | bytes 1179656 | tf_op jit(solution)/shard_map/ppermute | solution.py:177
  0.2 106.8 %collective-permute-start.6 = (bf16[192,1024]{1,0:T(8,128)(2,1)}, bf16[192,1024]{1,0:T(8,128)(2,1)S(1)}, u32[]{:S(2)}, u32[]{:S(2)}) collective-permute-start(bf16[192,1024]{1,0:T(8,128)(2,1)} %queries.1), channel_id=1, source_target_pairs={{0,8},{8,16},{16,24},{24,0},{1,9},{9,17},{17,25},{25,1},{2,10},{10... | collective-permute-start | bytes 1179656 | tf_op jit(solution)/shard_map/ppermute | solution.py:177
  5.0 3.9 %collective-permute-start = (bf16[400,128]{1,0:T(8,128)(2,1)S(1)}, bf16[400,128]{1,0:T(8,128)(2,1)S(1)}, u32[]{:S(2)}, u32[]{:S(2)}) collective-permute-start(bf16[400,128]{1,0:T(8,128)(2,1)S(1)} %pad_maximum_fusion.1), channel_id=1, source_target_pairs={{0,4},{4,0},{1,5},{5,1},{2,6},{6,2},{3,7},{7,3},{8,12},{12,8},{9,1... | collective-permute-start | bytes 307208 | tf_op jit(solution)/shard_map/ppermute | solution.py:177
  5.3 125.9 %collective-permute-start.10 = (bf16[1024,1024]{1,0:T(8,128)(2,1)}, bf16[1024,1024]{1,0:T(8,128)(2,1)}, u32[]{:S(2)}, u32[]{:S(2)}) collective-permute-start(bf16[1024,1024]{1,0:T(8,128)(2,1)} %param.9), channel_id=1, source_target_pairs={{0,4},{4,0},{1,5},{5,1},{2,6},{6,2},{3,7},{7,3},{8,12},{12,8},{9,1... | collective-permute-start | bytes 6291464 | tf_op jit(solution)/shard_map/ppermute | solution.py:177
  8.9 24.6 %collective-permute-start.1 = (bf16[2,400,128]{2,1,0:T(8,128)(2,1)S(1)}, bf16[2,400,128]{2,1,0:T(8,128)(2,1)S(1)}, u32[]{:S(2)}, u32[]{:S(2)}) collective-permute-start(bf16[2,400,128]{2,1,0:T(8,128)(2,1)S(1)} %bitcast_dynamic-update-slice_fusion.4), channel_id=1, source_target_pairs={{0,24},{8,0},{16,8},{24,16},{1,25},{9,1},{17,9},{25,17},{2,26},{10... | collective-permute-start | bytes 614408 | tf_op jit(solution)/shard_map/ppermute | solution.py:177
  33.4 16.6 %collective-permute-start.2 = (bf16[2,400,128]{2,1,0:T(8,128)(2,1)S(1)}, bf16[2,400,128]{2,1,0:T(8,128)(2,1)S(1)}, u32[]{:S(2)}, u32[]{:S(2)}) collective-permute-start(bf16[2,400,128]{2,1,0:T(8,128)(2,1)S(1)} %bitcast_dynamic-update-slice_fusion.4), channel_id=1, source_target_pairs={{0,16},{8,24},{16,0},{24,8},{1,17},{9,25},{17,1},{25,9},{2,18},{10... | collective-permute-start | bytes 614408 | tf_op jit(solution)/shard_map/ppermute | solution.py:177
  50.1 5.1 %collective-permute-start.3 = (bf16[2,400,128]{2,1,0:T(8,128)(2,1)S(1)}, bf16[2,400,128]{2,1,0:T(8,128)(2,1)S(1)}, u32[]{:S(2)}, u32[]{:S(2)}) collective-permute-start(bf16[2,400,128]{2,1,0:T(8,128)(2,1)S(1)} %bitcast_dynamic-update-slice_fusion.4), channel_id=1, source_target_pairs={{0,8},{8,16},{16,24},{24,0},{1,9},{9,17},{17,25},{25,1},{2,10},{10... | collective-permute-start | bytes 614408 | tf_op jit(solution)/shard_map/ppermute | solution.py:177
  85.7 0.7 copy-start.5
  95.1 0.7 copy-start.4
  95.8 29.1 %copy-start = (bf16[192,1024]{1,0:T(8,128)(2,1)S(1)}, bf16[192,1024]{1,0:T(8,128)(2,1)}, u32[]{:S(2)}) copy-start(bf16[192,1024]{1,0:T(8,128)(2,1)} %attend.4) | copy-start | bytes 1179652
  95.8 29.1 %copy-start.1 = (bf16[192,1024]{1,0:T(8,128)(2,1)S(1)}, bf16[192,1024]{1,0:T(8,128)(2,1)}, u32[]{:S(2)}) copy-start(bf16[192,1024]{1,0:T(8,128)(2,1)} %attend.5) | copy-start | bytes 1179652
  107.0 17.9 %copy-start.2 = (bf16[192,1024]{1,0:T(8,128)(2,1)S(1)}, bf16[192,1024]{1,0:T(8,128)(2,1)}, u32[]{:S(2)}) copy-start(bf16[192,1024]{1,0:T(8,128)(2,1)} %attend.6) | copy-start | bytes 1179652
  107.0 0.7 copy-start.3
  126.2 1.6 copy-start.6
  128.8 5.3 %collective-permute-start.7 = (bf16[384,1024]{1,0:T(8,128)(2,1)S(1)}, bf16[384,1024]{1,0:T(8,128)(2,1)S(1)}, u32[]{:S(2)}, u32[]{:S(2)}) collective-permute-start(bf16[384,1024]{1,0:T(8,128)(2,1)S(1)} %convolution_convert_fusion.2), channel_id=1, source_target_pairs={{0,1},{1,0},{2,3},{3,2},{4,5},{5,4},{6,7},{7,6},{8,9},{9,8},{10,11... | collective-permute-start | bytes 2359304 | tf_op jit(solution)/shard_map/ppermute | solution.py:245
  131.2 2.9 %copy-start.7 = (bf16[1024,1024]{1,0:T(8,128)(2,1)S(1)}, bf16[1024,1024]{1,0:T(8,128)(2,1)}, u32[]{:S(2)}) copy-start(bf16[1024,1024]{1,0:T(8,128)(2,1)} %param.9) | copy-start | bytes 6291460
  134.0 5.1 %collective-permute-start.11 = (bf16[384,1024]{1,0:T(8,128)(2,1)S(1)}, bf16[384,1024]{1,0:T(8,128)(2,1)S(1)}, u32[]{:S(2)}, u32[]{:S(2)}) collective-permute-start(bf16[384,1024]{1,0:T(8,128)(2,1)S(1)} %convolution_convert_fusion), channel_id=1, source_target_pairs={{0,1},{1,0},{2,3},{3,2},{4,5},{5,4},{6,7},{7,6},{8,9},{9,8},{10,11... | collective-permute-start | bytes 2359304 | tf_op jit(solution)/shard_map/ppermute | solution.py:245
  135.1 10.3 %collective-permute-start.8 = (bf16[192,1024]{1,0:T(8,128)(2,1)S(1)}, bf16[192,1024]{1,0:T(8,128)(2,1)S(1)}, u32[]{:S(2)}, u32[]{:S(2)}) collective-permute-start(bf16[192,1024]{1,0:T(8,128)(2,1)S(1)} %fusion.5), channel_id=1, source_target_pairs={{0,2},{1,3},{2,0},{3,1},{4,6},{5,7},{6,4},{7,5},{8,10},{9,11},{10,... | collective-permute-start | bytes 1179656 | tf_op jit(solution)/shard_map/ppermute | solution.py:245
  139.4 17.6 %collective-permute-start.12 = (bf16[192,1024]{1,0:T(8,128)(2,1)S(1)}, bf16[192,1024]{1,0:T(8,128)(2,1)S(1)}, u32[]{:S(2)}, u32[]{:S(2)}) collective-permute-start(bf16[192,1024]{1,0:T(8,128)(2,1)S(1)} %fusion.7), channel_id=1, source_target_pairs={{0,2},{1,3},{2,0},{3,1},{4,6},{5,7},{6,4},{7,5},{8,10},{9,11},{10,... | collective-permute-start | bytes 1179656 | tf_op jit(solution)/shard_map/ppermute | solution.py:245
  145.6 19.3 %collective-permute-start.9 = (bf16[192,1024]{1,0:T(8,128)(2,1)S(1)}, bf16[192,1024]{1,0:T(8,128)(2,1)S(1)}, u32[]{:S(2)}, u32[]{:S(2)}) collective-permute-start(bf16[192,1024]{1,0:T(8,128)(2,1)S(1)} %fusion.3), channel_id=1, source_target_pairs={{0,0},{1,8},{2,16},{3,24},{8,9},{9,17},{10,25},{11,1},{16,18},{17,... | collective-permute-start | bytes 1179656 | tf_op jit(solution)/shard_map/ppermute | solution.py:253
  157.1 20.4 %collective-permute-start.13 = (bf16[192,1024]{1,0:T(8,128)(2,1)S(1)}, bf16[192,1024]{1,0:T(8,128)(2,1)S(1)}, u32[]{:S(2)}, u32[]{:S(2)}) collective-permute-start(bf16[192,1024]{1,0:T(8,128)(2,1)S(1)} %fusion.2), channel_id=1, source_target_pairs={{0,0},{1,8},{2,16},{3,24},{8,9},{9,17},{10,25},{11,1},{16,18},{17,... | collective-permute-start | bytes 1179656 | tf_op jit(solution)/shard_map/ppermute | solution.py:253
